TPU v7x, 32 devices: a whole 2x2x4 slice. The times are simulated.
32 devices in a mesh: mesh: 8 (over z, x), field: 4 (over y, core).
Axes of the slice: x: 2, y: 2, z: 4, core: 2. Of those that a mesh axis runs over, the one named last changes fastest.
Arguments:
- velocity: float32 [3, 32, 1024], P(None, ('mesh', 'field')), may hold values from -4 to 4
- pressure: float32 [32, 1024], P(('mesh', 'field')), may hold values from -128 to 128
- fields: bfloat16 [3, 256, 32, 1024], P(None, 'field', 'mesh'), may hold values from -1.8 to 1.8
- brownian: bfloat16 [3, 256, 32, 1024], P(None, 'field', 'mesh'), may hold values from -4 to 4
Outputs:
- new_fields: bfloat16 [3, 256, 32, 1024], P(None, 'field', 'mesh')
- new_velocity: float32 [3, 32, 1024], P(None, ('mesh', 'field'))
All inputs are finite; a program needn't handle non-finite values.
Results may differ from a plain program's by a relative error of at most 0.001.
Values sent between devices are 32-bit elements; how exact they have to be, the bound alone decides.
A program may use at most 64 MiB of HBM per device.

v0:
```python
import functools

import jax
import jax.numpy as jnp
from jax import lax
from jax.experimental import pallas as pl
from jax.experimental.pallas import tpu as pltpu
from jax.sharding import PartitionSpec as P

NY = 32
NZ = 32
SWEEPS = 4
LANES = 128
CHUNKS = 4
VMEM_LIMIT = 24 * 1024 * 1024

time_step = 0.02
axial_weight = 400.0
transverse_weight = 40.0
weissenberg = 0.5
max_stretch = 50.0
polymer_viscosity = 40.0
noise_scale = (0.02 / 0.5) ** 0.5
diagonal_weight = 1.0 / 0.02 + 2.0 * 400.0 + 4.0 * 40.0
index_table = ((0, 1, 2), (1, 3, 4), (2, 4, 5))
component_pairs = ((0, 0), (0, 1), (0, 2), (1, 1), (1, 2), (2, 2))
diagonal_pairs = (0, 3, 5)


def plane_shifts(x):
    rows = x.shape[0]
    lane = lax.broadcasted_iota(jnp.int32, x.shape, 1)
    row = lax.broadcasted_iota(jnp.int32, x.shape, 0)
    column = lane % NZ
    ahead = pltpu.roll(x, LANES - NZ, 1)
    ahead_next = jnp.where(row == rows - 1, 0.0, pltpu.roll(ahead, rows - 1, 0))
    y_plus = jnp.where(lane >= LANES - NZ, ahead_next, ahead)
    behind = pltpu.roll(x, NZ, 1)
    behind_next = jnp.where(row == 0, 0.0, pltpu.roll(behind, 1, 0))
    y_minus = jnp.where(lane < NZ, behind_next, behind)
    z_plus = jnp.where(column < NZ - 1, pltpu.roll(x, LANES - 1, 1), 0.0)
    z_minus = jnp.where(column > 0, pltpu.roll(x, 1, 1), 0.0)
    return y_plus, y_minus, z_plus, z_minus


def step_kernel(
    subdomains, groups,
    vel, prs, fld, brn, advanced, out_base, out_flow, out_stress,
    cur, noise, base, grads, sums, vp, parts, got, stress,
    load_sem, flow_sem, vp_send, vp_recv, part_send, part_recv, st_send, st_recv,
):
    total = subdomains * groups
    halo = SWEEPS
    width = max(halo, groups)
    rows = vel.shape[1]
    count = fld.shape[1]
    packed = fld.shape[2]
    block = min(16, packed)
    chunk = count // CHUNKS
    sub = lax.axis_index("mesh")
    own = lax.axis_index("field")
    plane = sub * groups + own
    offsets = [d for d in range(-width, width + 1) if d != 0]

    def inside(d):
        return (plane + d >= 0) & (plane + d < total)

    def device(d):
        return ((plane + d) // groups, (plane + d) % groups)

    flow_loads = [
        pltpu.make_async_copy(vel, vp.at[width, pl.ds(0, 3)], flow_sem.at[0]),
        pltpu.make_async_copy(prs, vp.at[width, 3], flow_sem.at[1]),
    ]
    for copy in flow_loads:
        copy.start()
    barrier = pltpu.get_barrier_semaphore()
    partners = jnp.int32(0)
    for d in offsets:
        @pl.when(inside(d))
        def _(d=d):
            pl.semaphore_signal(
                barrier, inc=1, device_id=device(d), device_id_type=pl.DeviceIdType.MESH
            )
        partners = partners + jnp.where(inside(d), 1, 0)
    loads = []
    for number in range(CHUNKS):
        part = pl.ds(number * chunk, chunk)
        loads.append((
            pltpu.make_async_copy(fld.at[:, part], cur.at[:, part], load_sem.at[0, number]),
            pltpu.make_async_copy(brn.at[:, part], noise.at[:, part], load_sem.at[1, number]),
        ))
        for copy in loads[-1]:
            copy.start()
    for d in offsets:
        @pl.when(jnp.logical_not(inside(d)))
        def _(d=d):
            vp[width + d] = jnp.zeros(vp.shape[1:], jnp.float32)
            stress[width + d] = jnp.zeros(stress.shape[1:], jnp.float32)
    for copy in flow_loads:
        copy.wait()
    pl.semaphore_wait(barrier, partners)

    def flow_copy(d):
        return pltpu.make_async_remote_copy(
            src_ref=vp.at[width], dst_ref=vp.at[width - d],
            send_sem=vp_send.at[width + d], recv_sem=vp_recv.at[width - d],
            device_id=device(d), device_id_type=pl.DeviceIdType.MESH,
        )

    def urgent(d):
        ahead = (plane + d) // groups - sub
        return (
            (ahead == 0)
            | ((ahead == 1) & (own == groups - 1))
            | ((ahead == -1) & (own == 0))
        )

    for d in sorted(offsets, key=abs):
        @pl.when(inside(d) & urgent(d))
        def _(d=d):
            flow_copy(d).start()

    relax = time_step * max_stretch / (2.0 * weissenberg)
    for number in range(CHUNKS):
        for copy in loads[number]:
            copy.wait()

        @pl.loop(number * chunk, (number + 1) * chunk, unroll=2)
        def _(n):
            for start in range(0, packed, block):
                at = pl.ds(start, block)
                now = [cur[c, n, at].astype(jnp.float32) for c in range(3)]
                square = now[0] * now[0] + now[1] * now[1] + now[2] * now[2]
                keep = 1.0 - relax * (1.0 / (max_stretch - square))
                for c in range(3):
                    base[c, n, at] = now[c] * keep + noise_scale * noise[c, n, at].astype(jnp.float32)

    for d in sorted(offsets, key=abs):
        @pl.when(inside(d) & jnp.logical_not(urgent(d)))
        def _(d=d):
            flow_copy(d).start()

    def wait_flow(slot):
        pltpu.make_async_copy(vp.at[width], vp.at[slot], vp_recv.at[slot]).wait()

    for q in range(-1, groups + 1):
        d = q - own
        @pl.when((d != 0) & inside(d))
        def _(d=d):
            wait_flow(width + d)
    for q in range(groups):
        here = width + q - own
        at = pl.ds(q, rows, stride=groups)
        for a in range(3):
            centre = vp[here, a]
            y_plus, y_minus, z_plus, z_minus = plane_shifts(centre)
            scale = 0.5 * time_step
            grads[3 * a, at] = (vp[here + 1, a] - vp[here - 1, a]) * scale
            grads[3 * a + 1, at] = (y_plus - y_minus) * scale
            grads[3 * a + 2, at] = (z_plus - z_minus) * scale

    blocks = packed // block
    piece = block // groups

    def part_copy(number, r):
        to = (own + r) % groups
        return pltpu.make_async_remote_copy(
            src_ref=parts.at[number, to], dst_ref=got.at[number, r - 1],
            send_sem=part_send.at[number, r - 1], recv_sem=part_recv.at[number, r - 1],
            device_id=(sub, to), device_id_type=pl.DeviceIdType.MESH,
        )

    for start in range(0, packed, block):
        at = pl.ds(start, block)
        g = [grads[k, at] for k in range(9)]

        def one_field(n, acc):
            now = [cur[c, n, at].astype(jnp.float32) for c in range(3)]
            new = []
            for a in range(3):
                value = base[a, n, at] + (
                    g[3 * a] * now[0] + g[3 * a + 1] * now[1] + g[3 * a + 2] * now[2]
                )
                advanced[a, n, at] = value.astype(jnp.bfloat16)
                new.append(value)
            square = new[0] * new[0] + new[1] * new[1] + new[2] * new[2]
            inverse = 1.0 / (max_stretch - square)
            pulled = [inverse * value for value in new]
            return tuple(
                total_k + pulled[left] * new[right]
                for total_k, (left, right) in zip(acc, component_pairs)
            )

        zero = jnp.zeros((block, LANES), jnp.float32)
        acc = lax.fori_loop(0, count, one_field, (zero,) * 6, unroll=2)
        for k in range(6):
            sums[k, at] = acc[k]

        number = start // block
        for q in range(groups):
            for k in range(6):
                parts[number, q, pl.ds(k * piece, piece)] = sums[
                    k, pl.ds(start + q, piece, stride=groups)
                ]
        for r in range(1, groups):
            part_copy(number, r).start()

    for d in offsets:
        q = own + d
        @pl.when(inside(d) & ((q < -1) | (q > groups)))
        def _(d=d):
            wait_flow(width + d)
    reach = halo - 1
    for d in range(-halo, halo + 1):
        out_flow[halo + d] = vp[width + d, pl.ds(0, 3)]
    for d in range(-reach, reach + 1):
        here = width + d
        y_plus, y_minus, z_plus, z_minus = plane_shifts(vp[here, 3])
        slopes = (vp[here + 1, 3] - vp[here - 1, 3], y_plus - y_minus, z_plus - z_minus)
        for a in range(3):
            out_base[reach + d, a] = vp[here, a] * (1.0 / time_step) - 0.5 * slopes[a]

    factor = polymer_viscosity / weissenberg
    for number in range(blocks):
        summed = parts[number, own]
        for r in range(1, groups):
            part_copy(number, r).wait_recv()
            summed = summed + got[number, r - 1]
        value = summed * (factor * max_stretch / (count * groups))
        for k in range(6):
            of_pair = value[k * piece : (k + 1) * piece]
            if k in diagonal_pairs:
                of_pair = of_pair - factor
            stress[width, k, pl.ds(number * piece, piece)] = of_pair

    def stress_copy(d):
        parts_of = pl.ds(0, 3 if abs(d) == halo else 6)
        return pltpu.make_async_remote_copy(
            src_ref=stress.at[width, parts_of], dst_ref=stress.at[width - d, parts_of],
            send_sem=st_send.at[width + d], recv_sem=st_recv.at[width - d],
            device_id=device(d), device_id_type=pl.DeviceIdType.MESH,
        )

    near = [d for d in offsets if abs(d) <= halo]
    for d in sorted(near, key=abs):
        @pl.when(inside(d))
        def _(d=d):
            stress_copy(d).start()
    for d in sorted(near, key=abs):
        @pl.when(inside(d))
        def _(d=d):
            stress_copy(-d).wait_recv()

    for d in range(-halo, halo + 1):
        out_stress[halo + d] = stress[width + d]

    for d in offsets:
        @pl.when(inside(d))
        def _(d=d):
            flow_copy(d).wait_send()
            if abs(d) <= halo:
                stress_copy(d).wait_send()
    for number in range(blocks):
        for r in range(1, groups):
            part_copy(number, r).wait_send()


def momentum_kernel(
    subdomains, groups, advanced, source_base, flow, stress, out_fields, out_vel, vout, out_sem
):
    write = pltpu.make_async_copy(advanced, out_fields, out_sem.at[0])
    write.start()
    total = subdomains * groups
    halo = SWEEPS
    reach = halo - 1
    rows = flow.shape[2]
    plane = lax.axis_index("mesh") * groups + lax.axis_index("field")
    across = (
        lax.broadcasted_iota(jnp.int32, (rows, LANES), 0) * (LANES // NZ)
        + lax.broadcasted_iota(jnp.int32, (rows, LANES), 1) // NZ
    )
    solid = jnp.where((across < NY // 4) | (across >= NY - NY // 4), 1.0, 0.0)
    sources = {}
    fluid = {}
    for d in range(-reach, reach + 1):
        here = halo + d
        exists = jnp.where((plane + d >= 0) & (plane + d < total), 1.0 / diagonal_weight, 0.0)
        narrow = jnp.where(plane + d >= total // 2, 1.0, 0.0)
        fluid[d] = exists * (1.0 - narrow * solid)
        along_y = {}
        along_z = {}
        for k in range(1, 6):
            y_plus, y_minus, z_plus, z_minus = plane_shifts(stress[here, k])
            along_y[k] = y_plus - y_minus
            along_z[k] = z_plus - z_minus
        sources[d] = []
        for a in range(3):
            along_x = stress[here + 1, a] - stress[here - 1, a]
            slope = along_x + along_y[index_table[a][1]] + along_z[index_table[a][2]]
            sources[d].append(source_base[reach + d, a] + 0.5 * slope)

    for a in range(3):
        v = {d: flow[halo + d, a] for d in range(-halo, halo + 1)}
        for sweep in range(1, SWEEPS + 1):
            left = halo - sweep
            fresh = {}
            for d in range(-left, left + 1):
                y_plus, y_minus, z_plus, z_minus = plane_shifts(v[d])
                fresh[d] = fluid[d] * (
                    sources[d][a]
                    + axial_weight * (v[d + 1] + v[d - 1])
                    + transverse_weight * ((y_plus + y_minus) + (z_plus + z_minus))
                )
            v = fresh
        vout[a] = v[0]
    last = pltpu.make_async_copy(vout, out_vel, out_sem.at[1])
    last.start()
    write.wait()
    last.wait()


def body(subdomains, groups, velocity, pressure, fields, brownian):
    extent = velocity.shape[2]
    count, depth = fields.shape[1], fields.shape[2]
    rows = extent // LANES
    packed = rows * depth
    blocks = packed // min(16, packed)
    width = max(SWEEPS, groups)

    def pack(values):
        split = values.reshape(3, count, depth, rows, LANES)
        return split.transpose(0, 1, 3, 2, 4).reshape(3, count, packed, LANES)

    dma = pltpu.SemaphoreType.DMA
    near = pl.BlockSpec(memory_space=pltpu.VMEM)
    between = pl.pallas_call(
        functools.partial(step_kernel, subdomains, groups),
        out_shape=(
            pltpu.VMEM((3, count, packed, LANES), jnp.bfloat16),
            pltpu.VMEM((2 * SWEEPS - 1, 3, rows, LANES), jnp.float32),
            pltpu.VMEM((2 * SWEEPS + 1, 3, rows, LANES), jnp.float32),
            pltpu.VMEM((2 * SWEEPS + 1, 6, rows, LANES), jnp.float32),
        ),
        in_specs=[pl.BlockSpec(memory_space=pltpu.HBM)] * 4,
        out_specs=(near,) * 4,
        scratch_shapes=[
            pltpu.VMEM((3, count, packed, LANES), jnp.bfloat16),
            pltpu.VMEM((3, count, packed, LANES), jnp.bfloat16),
            pltpu.VMEM((3, count, packed, LANES), jnp.float32),
            pltpu.VMEM((9, packed, LANES), jnp.float32),
            pltpu.VMEM((6, packed, LANES), jnp.float32),
            pltpu.VMEM((2 * width + 1, 4, rows, LANES), jnp.float32),
            pltpu.VMEM((blocks, groups, 6 * rows // blocks, LANES), jnp.float32),
            pltpu.VMEM((blocks, groups - 1, 6 * rows // blocks, LANES), jnp.float32),
            pltpu.VMEM((2 * width + 1, 6, rows, LANES), jnp.float32),
            dma((2, CHUNKS)),
            dma((2,)),
            dma((2 * width + 1,)),
            dma((2 * width + 1,)),
            dma((blocks, groups - 1)),
            dma((blocks, groups - 1)),
            dma((2 * width + 1,)),
            dma((2 * width + 1,)),
        ],
        compiler_params=pltpu.CompilerParams(
            collective_id=0, has_side_effects=True, vmem_limit_bytes=VMEM_LIMIT
        ),
    )(
        *(
            pltpu.with_memory_space_constraint(values, pltpu.HBM)
            for values in (
                velocity.reshape(3, rows, LANES),
                pressure.reshape(rows, LANES),
                pack(fields),
                pack(brownian),
            )
        )
    )
    new_fields, new_velocity = pl.pallas_call(
        functools.partial(momentum_kernel, subdomains, groups),
        out_shape=(
            jax.ShapeDtypeStruct((3, count, packed, LANES), jnp.bfloat16),
            jax.ShapeDtypeStruct((3, rows, LANES), jnp.float32),
        ),
        in_specs=[near] * 4,
        out_specs=(pl.BlockSpec(memory_space=pltpu.HBM),) * 2,
        scratch_shapes=[pltpu.VMEM((3, rows, LANES), jnp.float32), dma((2,))],
        compiler_params=pltpu.CompilerParams(vmem_limit_bytes=VMEM_LIMIT),
    )(*between)
    unpacked = new_fields.reshape(3, count, rows, depth, LANES).transpose(0, 1, 3, 2, 4)
    return (
        unpacked.reshape(3, count, depth, extent),
        new_velocity.reshape(3, 1, extent),
    )


def solution(mesh):
    placed = (
        P(None, ("mesh", "field"), None),
        P(("mesh", "field"), None),
        P(None, "field", "mesh", None),
        P(None, "field", "mesh", None),
    )
    return jax.shard_map(
        functools.partial(body, mesh.shape["mesh"], mesh.shape["field"]),
        mesh=mesh,
        in_specs=placed,
        out_specs=(P(None, "field", "mesh", None), P(None, ("mesh", "field"), None)),
        check_vma=False,
    )
```

profile of v0, /device:TPU:0, one launch (start us, length us, event | category | flops | bytes accessed | tf_op | source)
XLA Modules:
  0.0 19.7 jit_solution(7130119807650533469)
XLA Ops:
  0.6 17.4 %shard_map.59 = (bf16[3,64,32,128]{3,2,1,0:T(8,128)(2,1)S(1)}, f32[7,3,8,128]{3,2,1,0:T(8,128)S(1)}, f32[9,3,8,128]{3,2,1,0:T(8,128)S(1)}, f32[9,6,8,128]{3,2,1,0:T(8,128)S(1)}) custom-call(f32[3,8,128]{2,1,0:T(8,128)} %bitcast.20, f32[8,128]{1,0:T(8,128)} %bitcast.21, bf16[3,64,32,128]{3,2,1,0:T(8,128)(2,1)} %bitcast.18, bf16[3,64,32,128]{3,2,1,0:T(8,128)(2,1)} %bitcast.19), custom_call_target="tpu_custom_call" | custom-call | tf_op jit(solution)/shard_map/pallas_call | solution.py:337
  18.1 1.6 %shard_map.60 = (bf16[3,64,32,128]{3,2,1,0:T(8,128)(2,1)}, f32[3,8,128]{2,1,0:T(8,128)}) custom-call(bf16[3,64,32,128]{3,2,1,0:T(8,128)(2,1)S(1)} %get-tuple-element.8.advanced, f32[7,3,8,128]{3,2,1,0:T(8,128)S(1)} %get-tuple-element.9.source_base, f32[9,3,8,128]{3,2,1,0:T(8,128)S(1)} %get-tuple-element.10.flow, f32[9,6,8,128]{3,2,1,0:T(8,128)S(1)} %get-tuple-element.11.stress), custom_call_target="tpu_custom_call" | custom-call | tf_op jit(solution)/shard_map/pallas_call | solution.py:380
where the time goes:
time: 19.9 us; the launch traced here: 19.7 us
  Pallas kernels  19.1 us (96%)
  between operations  0.64 us (3%)
    pallas_call x1, Pallas kernels, body(): pl.pallas_call(functools.partial(step_kernel, subdomains, groups), out_sh...  17.4 us
    pallas_call x1, Pallas kernels, body(): pl.pallas_call(functools.partial(momentum_kernel, subdomains, groups), ou...  1.62 us

commit v1 on v0

v1 whole, which is shorter than its diff:
```python
import functools

import jax
import jax.numpy as jnp
from jax import lax
from jax.experimental import pallas as pl
from jax.experimental.pallas import tpu as pltpu
from jax.sharding import PartitionSpec as P

NY = 32
NZ = 32
SWEEPS = 4
LANES = 128
CHUNKS = 4
EARLY_CHUNKS = 2
VMEM_LIMIT = 24 * 1024 * 1024

time_step = 0.02
axial_weight = 400.0
transverse_weight = 40.0
weissenberg = 0.5
max_stretch = 50.0
polymer_viscosity = 40.0
noise_scale = (0.02 / 0.5) ** 0.5
diagonal_weight = 1.0 / 0.02 + 2.0 * 400.0 + 4.0 * 40.0
index_table = ((0, 1, 2), (1, 3, 4), (2, 4, 5))
component_pairs = ((0, 0), (0, 1), (0, 2), (1, 1), (1, 2), (2, 2))
diagonal_pairs = (0, 3, 5)


def plane_shifts(x):
    rows = x.shape[0]
    lane = lax.broadcasted_iota(jnp.int32, x.shape, 1)
    row = lax.broadcasted_iota(jnp.int32, x.shape, 0)
    column = lane % NZ
    ahead = pltpu.roll(x, LANES - NZ, 1)
    ahead_next = jnp.where(row == rows - 1, 0.0, pltpu.roll(ahead, rows - 1, 0))
    y_plus = jnp.where(lane >= LANES - NZ, ahead_next, ahead)
    behind = pltpu.roll(x, NZ, 1)
    behind_next = jnp.where(row == 0, 0.0, pltpu.roll(behind, 1, 0))
    y_minus = jnp.where(lane < NZ, behind_next, behind)
    z_plus = jnp.where(column < NZ - 1, pltpu.roll(x, LANES - 1, 1), 0.0)
    z_minus = jnp.where(column > 0, pltpu.roll(x, 1, 1), 0.0)
    return y_plus, y_minus, z_plus, z_minus


def add(left, right):
    if left is None:
        return right
    return left if right is None else left + right


def step_kernel(
    subdomains, groups,
    vel, prs, fld, brn, advanced, out_vel,
    cur, noise, now32, next32, vbuf, pbuf, tx, rx,
    load_sem, flow_sem, vel_send, vel_mates, vel_cross, con_send, con_recv,
):
    rows = vel.shape[1]
    count = fld.shape[1]
    packed = fld.shape[2]
    total = subdomains * groups
    block = min(16, packed)
    chunk = count // CHUNKS
    reach = -(-SWEEPS // groups)
    spread = 2 * reach + 1
    sub = lax.axis_index("mesh")
    own = lax.axis_index("field")
    has_prev = sub > 0
    has_next = sub < subdomains - 1

    def inside(shift):
        return (sub + shift >= 0) & (sub + shift < subdomains)

    flow_loads = [
        pltpu.make_async_copy(vel, vbuf.at[own + 1], flow_sem.at[0]),
        pltpu.make_async_copy(prs, pbuf, flow_sem.at[1]),
    ]
    for copy in flow_loads:
        copy.start()

    barrier = pltpu.get_barrier_semaphore()

    def greet(device):
        pl.semaphore_signal(
            barrier, inc=1, device_id=device, device_id_type=pl.DeviceIdType.MESH
        )

    @pl.when(has_next)
    def _():
        greet((sub + 1, 0))

    @pl.when(has_prev)
    def _():
        greet((sub - 1, groups - 1))

    for r in range(1, groups):
        greet((sub, (own + r) % groups))

    loads = []
    for number in range(CHUNKS):
        part = pl.ds(number * chunk, chunk)
        loads.append((
            pltpu.make_async_copy(fld.at[:, part], cur.at[:, part], load_sem.at[0, number]),
            pltpu.make_async_copy(brn.at[:, part], noise.at[:, part], load_sem.at[1, number]),
        ))
        for copy in loads[-1]:
            copy.start()

    @pl.when(jnp.logical_not(has_prev))
    def _():
        vbuf[0] = jnp.zeros(vbuf.shape[1:], jnp.float32)

    @pl.when(jnp.logical_not(has_next))
    def _():
        vbuf[groups + 1] = jnp.zeros(vbuf.shape[1:], jnp.float32)

    for shift in range(-reach, reach + 1):
        if shift != 0:
            @pl.when(jnp.logical_not(inside(shift)))
            def _(shift=shift):
                rx[pl.ds((reach + shift) * groups, groups)] = jnp.zeros(
                    (groups,) + rx.shape[1:], jnp.float32
                )

    relax = time_step * max_stretch / (2.0 * weissenberg)

    def base_chunk(number):
        for copy in loads[number]:
            copy.wait()

        @pl.loop(number * chunk, (number + 1) * chunk, unroll=2)
        def _(n):
            for start in range(0, packed, block):
                at = pl.ds(start, block)
                now = [cur[c, n, at].astype(jnp.float32) for c in range(3)]
                square = now[0] * now[0] + now[1] * now[1] + now[2] * now[2]
                keep = 1.0 - relax * (1.0 / (max_stretch - square))
                for c in range(3):
                    now32[c, n, at] = now[c]
                    next32[c, n, at] = now[c] * keep + noise_scale * noise[c, n, at].astype(jnp.float32)

    for number in range(EARLY_CHUNKS):
        base_chunk(number)

    for copy in flow_loads:
        copy.wait()
    sends_prev = (own == 0) & has_prev
    sends_next = (own == groups - 1) & has_next
    greetings = groups - 1 + jnp.where(sends_prev, groups, 0) + jnp.where(sends_next, groups, 0)
    pl.semaphore_wait(barrier, greetings)

    def flow_copy(device, slot, recv):
        return pltpu.make_async_remote_copy(
            src_ref=vbuf.at[own + 1], dst_ref=vbuf.at[slot],
            send_sem=vel_send.at[0], recv_sem=recv,
            device_id=device, device_id_type=pl.DeviceIdType.MESH,
        )

    @pl.when(sends_prev)
    def _():
        for f in reversed(range(groups)):
            flow_copy((sub - 1, f), groups + 1, vel_cross.at[1]).start()

    @pl.when(sends_next)
    def _():
        for f in range(groups):
            flow_copy((sub + 1, f), 0, vel_cross.at[0]).start()

    for r in range(1, groups):
        flow_copy((sub, (own + r) % groups), own + 1, vel_mates.at[0]).start()

    for number in range(EARLY_CHUNKS, CHUNKS):
        base_chunk(number)

    factor = polymer_viscosity / weissenberg
    stress = {}

    def plane_fields(q):
        scale = 0.5 * time_step
        g = [None] * 9
        for a in range(3):
            y_plus, y_minus, z_plus, z_minus = plane_shifts(vbuf[q + 1, a])
            g[3 * a] = (vbuf[q + 2, a] - vbuf[q, a]) * scale
            g[3 * a + 1] = (y_plus - y_minus) * scale
            g[3 * a + 2] = (z_plus - z_minus) * scale
        at = pl.ds(q, rows, stride=groups)

        def one_field(n, acc):
            now = [now32[c, n, at] for c in range(3)]
            new = []
            for a in range(3):
                value = next32[a, n, at] + (
                    g[3 * a] * now[0] + g[3 * a + 1] * now[1] + g[3 * a + 2] * now[2]
                )
                next32[a, n, at] = value
                new.append(value)
            square = new[0] * new[0] + new[1] * new[1] + new[2] * new[2]
            inverse = 1.0 / (max_stretch - square)
            pulled = [inverse * value for value in new]
            return tuple(
                total_k + pulled[left] * new[right]
                for total_k, (left, right) in zip(acc, component_pairs)
            )

        zero = jnp.zeros((rows, LANES), jnp.float32)
        acc = lax.fori_loop(0, count, one_field, (zero,) * 6, unroll=2)
        for k in range(6):
            value = acc[k] * (factor * max_stretch / (count * groups))
            stress[q, k] = value - factor / groups if k in diagonal_pairs else value

    pltpu.make_async_copy(
        vbuf.at[pl.ds(0, groups - 1)], vbuf.at[pl.ds(0, groups - 1)], vel_mates.at[0]
    ).wait()
    for q in range(1, groups - 1):
        plane_fields(q)

    @pl.when(has_prev)
    def _():
        pltpu.make_async_copy(vbuf.at[0], vbuf.at[0], vel_cross.at[0]).wait()

    plane_fields(0)

    @pl.when(has_next)
    def _():
        pltpu.make_async_copy(vbuf.at[0], vbuf.at[0], vel_cross.at[1]).wait()

    plane_fields(groups - 1)

    across = (
        lax.broadcasted_iota(jnp.int32, (rows, LANES), 0) * (LANES // NZ)
        + lax.broadcasted_iota(jnp.int32, (rows, LANES), 1) // NZ
    )
    solid = jnp.where((across < NY // 4) | (across >= NY - NY // 4), 1.0, 0.0)
    first, last = -reach * groups, groups - 1 + reach * groups
    fluid = {}
    for d in range(first, last + 1):
        plane = sub * groups + d
        exists = jnp.where((plane >= 0) & (plane < total), 1.0 / diagonal_weight, 0.0)
        narrow = jnp.where(plane >= total // 2, 1.0, 0.0)
        fluid[d] = exists * (1.0 - narrow * solid)

    mine = [jnp.where(own == q, 1.0, 0.0) for q in range(groups)]
    own_vel = [vbuf[own + 1, a] for a in range(3)]
    own_prs = pbuf[...]
    y_plus, y_minus, z_plus, z_minus = plane_shifts(own_prs)
    own_source = [
        own_vel[0] * (1.0 / time_step),
        own_vel[1] * (1.0 / time_step) - 0.5 * (y_plus - y_minus),
        own_vel[2] * (1.0 / time_step) - 0.5 * (z_plus - z_minus),
    ]
    sources = {}
    for d in range(-1, groups + 1):
        along_y = {}
        along_z = {}
        if 0 <= d < groups:
            for k in range(1, 6):
                y_plus, y_minus, z_plus, z_minus = plane_shifts(stress[d, k])
                along_y[k] = y_plus - y_minus
                along_z[k] = z_plus - z_minus
        for a in range(3):
            slope = None
            if 0 <= d + 1 < groups:
                above = stress[d + 1, a]
                if a == 0:
                    above = above - mine[d + 1] * own_prs
                slope = above
            if 0 <= d - 1 < groups:
                below = stress[d - 1, a]
                if a == 0:
                    below = below - mine[d - 1] * own_prs
                slope = -below if slope is None else slope - below
            if 0 <= d < groups:
                slope = slope + along_y[index_table[a][1]] + along_z[index_table[a][2]]
            value = 0.5 * slope
            if 0 <= d < groups:
                value = value + mine[d] * own_source[a]
            sources[d, a] = value

    for a in range(3):
        v = {q: mine[q] * own_vel[a] for q in range(groups)}
        for sweep in range(1, SWEEPS + 1):
            fresh = {}
            for d in range(-sweep, groups + sweep):
                value = sources.get((d, a))
                if d + 1 in v or d - 1 in v:
                    value = add(value, axial_weight * add(v.get(d + 1), v.get(d - 1)))
                if d in v:
                    y_plus, y_minus, z_plus, z_minus = plane_shifts(v[d])
                    value = add(
                        value,
                        transverse_weight * ((y_plus + y_minus) + (z_plus + z_minus)),
                    )
                fresh[d] = fluid[d] * value
            v = fresh
        for d in range(first, last + 1):
            tx[d - first, a] = v[d] if d in v else jnp.zeros((rows, LANES), jnp.float32)

    def share(shift, f):
        return pltpu.make_async_remote_copy(
            src_ref=tx.at[(reach + shift) * groups + f],
            dst_ref=rx.at[(reach - shift) * groups + own],
            send_sem=con_send.at[0], recv_sem=con_recv.at[0],
            device_id=(sub + shift, f), device_id_type=pl.DeviceIdType.MESH,
        )

    for shift in range(-reach, reach + 1):
        if shift != 0:
            @pl.when(inside(shift))
            def _(shift=shift):
                for r in range(groups):
                    share(shift, (own + r) % groups).start()
        else:
            for r in range(1, groups):
                share(0, (own + r) % groups).start()

    here = reach * groups + own
    rx[here] = tx[here]

    @pl.loop(0, count, unroll=2)
    def _(n):
        for c in range(3):
            for start in range(0, packed, block):
                at = pl.ds(start, block)
                advanced[c, n, at] = next32[c, n, at].astype(jnp.bfloat16)

    partners = groups - 1
    for shift in range(-reach, reach + 1):
        if shift != 0:
            partners = partners + jnp.where(inside(shift), groups, 0)
    sent_flow = groups - 1 + jnp.where(sends_prev, groups, 0) + jnp.where(sends_next, groups, 0)

    def wait_planes(number, options, sem):
        for option in options:
            @pl.when(number == option)
            def _(option=option):
                planes = rx.at[pl.ds(0, option)]
                pltpu.make_async_copy(planes, planes, sem).wait()

    flow_options = [groups - 1 + k * groups for k in range(3)]
    share_options = [groups - 1 + k * groups for k in range(spread)]
    wait_planes(sent_flow, flow_options, vel_send.at[0])
    wait_planes(partners, share_options, con_recv.at[0])
    for a in range(3):
        value = rx[0, a]
        for k in range(1, spread * groups):
            value = value + rx[k, a]
        out_vel[a] = value
    wait_planes(partners, share_options, con_send.at[0])


def write_kernel(advanced, velocity, out_fields, out_vel, out_sem):
    copies = [
        pltpu.make_async_copy(velocity, out_vel, out_sem.at[1]),
        pltpu.make_async_copy(advanced, out_fields, out_sem.at[0]),
    ]
    for copy in copies:
        copy.start()
    for copy in copies:
        copy.wait()


def body(subdomains, groups, velocity, pressure, fields, brownian):
    extent = velocity.shape[2]
    count, depth = fields.shape[1], fields.shape[2]
    rows = extent // LANES
    packed = rows * depth
    slots = (2 * (-(-SWEEPS // groups)) + 1) * groups

    def pack(values):
        split = values.reshape(3, count, depth, rows, LANES)
        return split.transpose(0, 1, 3, 2, 4).reshape(3, count, packed, LANES)

    dma = pltpu.SemaphoreType.DMA
    near = pl.BlockSpec(memory_space=pltpu.VMEM)
    between = pl.pallas_call(
        functools.partial(step_kernel, subdomains, groups),
        out_shape=(
            pltpu.VMEM((3, count, packed, LANES), jnp.bfloat16),
            pltpu.VMEM((3, rows, LANES), jnp.float32),
        ),
        in_specs=[pl.BlockSpec(memory_space=pltpu.HBM)] * 4,
        out_specs=(near,) * 2,
        scratch_shapes=[
            pltpu.VMEM((3, count, packed, LANES), jnp.bfloat16),
            pltpu.VMEM((3, count, packed, LANES), jnp.bfloat16),
            pltpu.VMEM((3, count, packed, LANES), jnp.float32),
            pltpu.VMEM((3, count, packed, LANES), jnp.float32),
            pltpu.VMEM((groups + 2, 3, rows, LANES), jnp.float32),
            pltpu.VMEM((rows, LANES), jnp.float32),
            pltpu.VMEM((slots, 3, rows, LANES), jnp.float32),
            pltpu.VMEM((slots, 3, rows, LANES), jnp.float32),
            dma((2, CHUNKS)),
            dma((2,)),
            dma((1,)),
            dma((1,)),
            dma((2,)),
            dma((1,)),
            dma((1,)),
        ],
        compiler_params=pltpu.CompilerParams(
            collective_id=0, has_side_effects=True, vmem_limit_bytes=VMEM_LIMIT
        ),
    )(
        *(
            pltpu.with_memory_space_constraint(values, pltpu.HBM)
            for values in (
                velocity.reshape(3, rows, LANES),
                pressure.reshape(rows, LANES),
                pack(fields),
                pack(brownian),
            )
        )
    )
    new_fields, new_velocity = pl.pallas_call(
        write_kernel,
        out_shape=(
            jax.ShapeDtypeStruct((3, count, packed, LANES), jnp.bfloat16),
            jax.ShapeDtypeStruct((3, rows, LANES), jnp.float32),
        ),
        in_specs=[near] * 2,
        out_specs=(pl.BlockSpec(memory_space=pltpu.HBM),) * 2,
        scratch_shapes=[dma((2,))],
        compiler_params=pltpu.CompilerParams(vmem_limit_bytes=VMEM_LIMIT),
    )(*between)
    unpacked = new_fields.reshape(3, count, rows, depth, LANES).transpose(0, 1, 3, 2, 4)
    return (
        unpacked.reshape(3, count, depth, extent),
        new_velocity.reshape(3, 1, extent),
    )


def solution(mesh):
    placed = (
        P(None, ("mesh", "field"), None),
        P(("mesh", "field"), None),
        P(None, "field", "mesh", None),
        P(None, "field", "mesh", None),
    )
    return jax.shard_map(
        functools.partial(body, mesh.shape["mesh"], mesh.shape["field"]),
        mesh=mesh,
        in_specs=placed,
        out_specs=(P(None, "field", "mesh", None), P(None, ("mesh", "field"), None)),
        check_vma=False,
    )
```

time: 19.9 us -> 15.9 us (0.80)
  Pallas kernels: 19.1 us -> 15.1 us
    pallas_call x1, Pallas kernels: 17.4 us -> 13.9 us  [body(): pl.pallas_call(functools.partial(step_kernel, subdomains, groups), out_sh...]
    pallas_call x1, Pallas kernels: 1.62 us -> 1.17 us  [body(): pl.pallas_call(write_kernel, out_shape=(jax.ShapeDtypeStruct((3, count, p...]
where the time goes in v1:
time: 15.9 us; the launch traced here: 15.7 us
  Pallas kernels  15.1 us (95%)
  between operations  0.64 us (4%)
    pallas_call x1, Pallas kernels, body(): pl.pallas_call(functools.partial(step_kernel, subdomains, groups), out_sh...  13.9 us
    pallas_call x1, Pallas kernels, body(): pl.pallas_call(write_kernel, out_shape=(jax.ShapeDtypeStruct((3, count, p...  1.17 us

profile of v1, /device:TPU:0, one launch (start us, length us, event | category | flops | bytes accessed | tf_op | source)
XLA Modules:
  0.0 15.7 jit_solution(5010318267983236727)
XLA Ops:
  0.6 13.9 %shard_map.59 = (bf16[3,64,32,128]{3,2,1,0:T(8,128)(2,1)S(1)}, f32[3,8,128]{2,1,0:T(8,128)S(1)}) custom-call(f32[3,8,128]{2,1,0:T(8,128)} %bitcast.20, f32[8,128]{1,0:T(8,128)} %bitcast.21, bf16[3,64,32,128]{3,2,1,0:T(8,128)(2,1)} %bitcast.18, bf16[3,64,32,128]{3,2,1,0:T(8,128)(2,1)} %bitcast.19), custom_call_target="tpu_custom_call" | custom-call | tf_op jit(solution)/shard_map/pallas_call | solution.py:376
  14.5 1.2 %shard_map.60 = (bf16[3,64,32,128]{3,2,1,0:T(8,128)(2,1)}, f32[3,8,128]{2,1,0:T(8,128)}) custom-call(bf16[3,64,32,128]{3,2,1,0:T(8,128)(2,1)S(1)} %get-tuple-element.6.advanced, f32[3,8,128]{2,1,0:T(8,128)S(1)} %get-tuple-element.7.velocity), custom_call_target="tpu_custom_call" | custom-call | tf_op jit(solution)/shard_map/pallas_call | solution.py:415

commit v2 on v1

--- a/solution.py
+++ b/solution.py
@@ -12,7 +12,7 @@
 SWEEPS = 4
 LANES = 128
 CHUNKS = 4
-EARLY_CHUNKS = 2
+EARLY_CHUNKS = 0
 VMEM_LIMIT = 24 * 1024 * 1024
 
 time_step = 0.02
@@ -204,7 +204,7 @@
             )
 
         zero = jnp.zeros((rows, LANES), jnp.float32)
-        acc = lax.fori_loop(0, count, one_field, (zero,) * 6, unroll=2)
+        acc = lax.fori_loop(0, count, one_field, (zero,) * 6, unroll=8)
         for k in range(6):
             value = acc[k] * (factor * max_stretch / (count * groups))
             stress[q, k] = value - factor / groups if k in diagonal_pairs else value
@@ -239,6 +239,7 @@
         exists = jnp.where((plane >= 0) & (plane < total), 1.0 / diagonal_weight, 0.0)
         narrow = jnp.where(plane >= total // 2, 1.0, 0.0)
         fluid[d] = exists * (1.0 - narrow * solid)
+    pull = {d: value * transverse_weight for d, value in fluid.items()}
 
     mine = [jnp.where(own == q, 1.0, 0.0) for q in range(groups)]
     own_vel = [vbuf[own + 1, a] for a in range(3)]
@@ -277,24 +278,24 @@
                 value = value + mine[d] * own_source[a]
             sources[d, a] = value
 
-    for a in range(3):
-        v = {q: mine[q] * own_vel[a] for q in range(groups)}
-        for sweep in range(1, SWEEPS + 1):
-            fresh = {}
-            for d in range(-sweep, groups + sweep):
-                value = sources.get((d, a))
-                if d + 1 in v or d - 1 in v:
-                    value = add(value, axial_weight * add(v.get(d + 1), v.get(d - 1)))
-                if d in v:
-                    y_plus, y_minus, z_plus, z_minus = plane_shifts(v[d])
-                    value = add(
-                        value,
-                        transverse_weight * ((y_plus + y_minus) + (z_plus + z_minus)),
-                    )
-                fresh[d] = fluid[d] * value
-            v = fresh
-        for d in range(first, last + 1):
-            tx[d - first, a] = v[d] if d in v else jnp.zeros((rows, LANES), jnp.float32)
+    v = {(q, a): mine[q] * own_vel[a] for q in range(groups) for a in range(3)}
+    scaled = {(d, a): fluid[d] * value for (d, a), value in sources.items()}
+    ratio = axial_weight / transverse_weight
+    for sweep in range(1, SWEEPS + 1):
+        fresh = {}
+        for d in range(-sweep, groups + sweep):
+            for a in range(3):
+                value = add(v.get((d + 1, a)), v.get((d - 1, a)))
+                if value is not None:
+                    value = value * ratio
+                if (d, a) in v:
+                    y_plus, y_minus, z_plus, z_minus = plane_shifts(v[d, a])
+                    value = add(value, (y_plus + y_minus) + (z_plus + z_minus))
+                fresh[d, a] = add(scaled.get((d, a)), pull[d] * value)
+        v = fresh
+    for d in range(first, last + 1):
+        for a in range(3):
+            tx[d - first, a] = v[d, a] if (d, a) in v else jnp.zeros((rows, LANES), jnp.float32)
 
     def share(shift, f):
         return pltpu.make_async_remote_copy(

time: 15.9 us -> 14.7 us (0.925)
  Pallas kernels: 15.1 us -> 13.8 us
    pallas_call x1, Pallas kernels: 13.9 us -> 12.7 us  [body(): pl.pallas_call(functools.partial(step_kernel, subdomains, groups), out_sh...]
where the time goes in v2:
time: 14.7 us; the launch traced here: 14.5 us
  Pallas kernels  13.8 us (94%)
  between operations  0.64 us (4%)
    pallas_call x1, Pallas kernels, body(): pl.pallas_call(functools.partial(step_kernel, subdomains, groups), out_sh...  12.7 us
    pallas_call x1, Pallas kernels, body(): pl.pallas_call(write_kernel, out_shape=(jax.ShapeDtypeStruct((3, count, p...  1.17 us

profile of v2, /device:TPU:0, one launch (start us, length us, event | category | flops | bytes accessed | tf_op | source)
XLA Modules:
  0.0 14.5 jit_solution(7991224226103606663)
XLA Ops:
  0.6 12.7 %shard_map.59 = (bf16[3,64,32,128]{3,2,1,0:T(8,128)(2,1)S(1)}, f32[3,8,128]{2,1,0:T(8,128)S(1)}) custom-call(f32[3,8,128]{2,1,0:T(8,128)} %bitcast.20, f32[8,128]{1,0:T(8,128)} %bitcast.21, bf16[3,64,32,128]{3,2,1,0:T(8,128)(2,1)} %bitcast.18, bf16[3,64,32,128]{3,2,1,0:T(8,128)(2,1)} %bitcast.19), custom_call_target="tpu_custom_call" | custom-call | tf_op jit(solution)/shard_map/pallas_call | solution.py:377
  13.3 1.2 %shard_map.60 = (bf16[3,64,32,128]{3,2,1,0:T(8,128)(2,1)}, f32[3,8,128]{2,1,0:T(8,128)}) custom-call(bf16[3,64,32,128]{3,2,1,0:T(8,128)(2,1)S(1)} %get-tuple-element.6.advanced, f32[3,8,128]{2,1,0:T(8,128)S(1)} %get-tuple-element.7.velocity), custom_call_target="tpu_custom_call" | custom-call | tf_op jit(solution)/shard_map/pallas_call | solution.py:416

commit v3 on v2

--- a/solution.py
+++ b/solution.py
@@ -13,6 +13,7 @@
 LANES = 128
 CHUNKS = 4
 EARLY_CHUNKS = 0
+UNROLL = 32
 VMEM_LIMIT = 24 * 1024 * 1024
 
 time_step = 0.02
@@ -53,8 +54,8 @@
 def step_kernel(
     subdomains, groups,
     vel, prs, fld, brn, advanced, out_vel,
-    cur, noise, now32, next32, vbuf, pbuf, tx, rx,
-    load_sem, flow_sem, vel_send, vel_mates, vel_cross, con_send, con_recv,
+    cur, noise, now32, next32, vbuf, pbuf, grads, tx, rx,
+    load_sem, flow_sem, vel_send, vel_mates, vel_cross, con_send, con_recv, ready,
 ):
     rows = vel.shape[1]
     count = fld.shape[1]
@@ -94,17 +95,17 @@
     def _():
         greet((sub - 1, groups - 1))
 
-    for r in range(1, groups):
-        greet((sub, (own + r) % groups))
-
-    loads = []
+    for helper in range(1, groups - 1):
+        @pl.when(own != helper)
+        def _(helper=helper):
+            greet((sub, helper))
+
     for number in range(CHUNKS):
         part = pl.ds(number * chunk, chunk)
-        loads.append((
-            pltpu.make_async_copy(fld.at[:, part], cur.at[:, part], load_sem.at[0, number]),
-            pltpu.make_async_copy(brn.at[:, part], noise.at[:, part], load_sem.at[1, number]),
-        ))
-        for copy in loads[-1]:
+        for copy in (
+            pltpu.make_async_copy(fld.at[:, part], cur.at[:, part], load_sem.at[number]),
+            pltpu.make_async_copy(brn.at[:, part], noise.at[:, part], load_sem.at[number]),
+        ):
             copy.start()
 
     @pl.when(jnp.logical_not(has_prev))
@@ -126,8 +127,8 @@
     relax = time_step * max_stretch / (2.0 * weissenberg)
 
     def base_chunk(number):
-        for copy in loads[number]:
-            copy.wait()
+        both = pl.ds(0, 2 * chunk)
+        pltpu.make_async_copy(fld.at[:, both], cur.at[:, both], load_sem.at[number]).wait()
 
         @pl.loop(number * chunk, (number + 1) * chunk, unroll=2)
         def _(n):
@@ -147,8 +148,25 @@
         copy.wait()
     sends_prev = (own == 0) & has_prev
     sends_next = (own == groups - 1) & has_next
-    greetings = groups - 1 + jnp.where(sends_prev, groups, 0) + jnp.where(sends_next, groups, 0)
-    pl.semaphore_wait(barrier, greetings)
+    edge = (own == 0) | (own == groups - 1)
+
+    @pl.when(jnp.logical_not(edge))
+    def _():
+        pl.semaphore_wait(barrier, groups - 1)
+
+    def admit(helper, device):
+        @pl.when(own == helper)
+        def _():
+            pl.semaphore_signal(
+                ready, inc=1, device_id=(sub, device), device_id_type=pl.DeviceIdType.MESH
+            )
+
+    admit(1, 0)
+    admit(groups - 2, groups - 1)
+
+    @pl.when(edge)
+    def _():
+        pl.semaphore_wait(ready, 1)
 
     def flow_copy(device, slot, recv):
         return pltpu.make_async_remote_copy(
@@ -157,33 +175,35 @@
             device_id=device, device_id_type=pl.DeviceIdType.MESH,
         )
 
+    for r in range(1, groups):
+        flow_copy((sub, (own + r) % groups), own + 1, vel_mates.at[0]).start()
+
     @pl.when(sends_prev)
     def _():
+        pl.semaphore_wait(barrier, groups)
         for f in reversed(range(groups)):
             flow_copy((sub - 1, f), groups + 1, vel_cross.at[1]).start()
 
     @pl.when(sends_next)
     def _():
+        pl.semaphore_wait(barrier, groups)
         for f in range(groups):
             flow_copy((sub + 1, f), 0, vel_cross.at[0]).start()
 
-    for r in range(1, groups):
-        flow_copy((sub, (own + r) % groups), own + 1, vel_mates.at[0]).start()
-
     for number in range(EARLY_CHUNKS, CHUNKS):
         base_chunk(number)
 
     factor = polymer_viscosity / weissenberg
     stress = {}
 
+    scale = 0.5 * time_step
+
     def plane_fields(q):
-        scale = 0.5 * time_step
         g = [None] * 9
         for a in range(3):
-            y_plus, y_minus, z_plus, z_minus = plane_shifts(vbuf[q + 1, a])
             g[3 * a] = (vbuf[q + 2, a] - vbuf[q, a]) * scale
-            g[3 * a + 1] = (y_plus - y_minus) * scale
-            g[3 * a + 2] = (z_plus - z_minus) * scale
+            g[3 * a + 1] = grads[q, a]
+            g[3 * a + 2] = grads[q, 3 + a]
         at = pl.ds(q, rows, stride=groups)
 
         def one_field(n, acc):
@@ -204,7 +224,7 @@
             )
 
         zero = jnp.zeros((rows, LANES), jnp.float32)
-        acc = lax.fori_loop(0, count, one_field, (zero,) * 6, unroll=8)
+        acc = lax.fori_loop(0, count, one_field, (zero,) * 6, unroll=UNROLL)
         for k in range(6):
             value = acc[k] * (factor * max_stretch / (count * groups))
             stress[q, k] = value - factor / groups if k in diagonal_pairs else value
@@ -212,6 +232,11 @@
     pltpu.make_async_copy(
         vbuf.at[pl.ds(0, groups - 1)], vbuf.at[pl.ds(0, groups - 1)], vel_mates.at[0]
     ).wait()
+    for q in range(groups):
+        for a in range(3):
+            y_plus, y_minus, z_plus, z_minus = plane_shifts(vbuf[q + 1, a])
+            grads[q, a] = (y_plus - y_minus) * scale
+            grads[q, 3 + a] = (z_plus - z_minus) * scale
     for q in range(1, groups - 1):
         plane_fields(q)
 
@@ -305,12 +330,14 @@
             device_id=(sub + shift, f), device_id_type=pl.DeviceIdType.MESH,
         )
 
+    half = max(1, groups // 2)
+    across_first = (own // half + 1) * half
     for shift in range(-reach, reach + 1):
         if shift != 0:
             @pl.when(inside(shift))
             def _(shift=shift):
                 for r in range(groups):
-                    share(shift, (own + r) % groups).start()
+                    share(shift, (across_first + r) % groups).start()
         else:
             for r in range(1, groups):
                 share(0, (own + r) % groups).start()
@@ -389,15 +416,17 @@
             pltpu.VMEM((3, count, packed, LANES), jnp.float32),
             pltpu.VMEM((groups + 2, 3, rows, LANES), jnp.float32),
             pltpu.VMEM((rows, LANES), jnp.float32),
+            pltpu.VMEM((groups, 6, rows, LANES), jnp.float32),
             pltpu.VMEM((slots, 3, rows, LANES), jnp.float32),
             pltpu.VMEM((slots, 3, rows, LANES), jnp.float32),
-            dma((2, CHUNKS)),
+            dma((CHUNKS,)),
             dma((2,)),
             dma((1,)),
             dma((1,)),
             dma((2,)),
             dma((1,)),
             dma((1,)),
+            pltpu.SemaphoreType.REGULAR,
         ],
         compiler_params=pltpu.CompilerParams(
             collective_id=0, has_side_effects=True, vmem_limit_bytes=VMEM_LIMIT

time: 14.7 us -> 14.3 us (0.973)
  Pallas kernels: 13.8 us -> 13.4 us
    pallas_call x1, Pallas kernels: 12.7 us -> 12.3 us  [body(): pl.pallas_call(functools.partial(step_kernel, subdomains, groups), out_sh...]
where the time goes in v3:
time: 14.3 us; the launch traced here: 14.1 us
  Pallas kernels  13.4 us (94%)
  between operations  0.64 us (4%)
    pallas_call x1, Pallas kernels, body(): pl.pallas_call(functools.partial(step_kernel, subdomains, groups), out_sh...  12.3 us
    pallas_call x1, Pallas kernels, body(): pl.pallas_call(write_kernel, out_shape=(jax.ShapeDtypeStruct((3, count, p...  1.17 us

profile of v3, /device:TPU:0, one launch (start us, length us, event | category | flops | bytes accessed | tf_op | source)
XLA Modules:
  0.0 14.1 jit_solution(7714687138315704356)
XLA Ops:
  0.6 12.3 %shard_map.59 = (bf16[3,64,32,128]{3,2,1,0:T(8,128)(2,1)S(1)}, f32[3,8,128]{2,1,0:T(8,128)S(1)}) custom-call(f32[3,8,128]{2,1,0:T(8,128)} %bitcast.20, f32[8,128]{1,0:T(8,128)} %bitcast.21, bf16[3,64,32,128]{3,2,1,0:T(8,128)(2,1)} %bitcast.18, bf16[3,64,32,128]{3,2,1,0:T(8,128)(2,1)} %bitcast.19), custom_call_target="tpu_custom_call" | custom-call | tf_op jit(solution)/shard_map/pallas_call | solution.py:404
  12.9 1.2 %shard_map.60 = (bf16[3,64,32,128]{3,2,1,0:T(8,128)(2,1)}, f32[3,8,128]{2,1,0:T(8,128)}) custom-call(bf16[3,64,32,128]{3,2,1,0:T(8,128)(2,1)S(1)} %get-tuple-element.6.advanced, f32[3,8,128]{2,1,0:T(8,128)S(1)} %get-tuple-element.7.velocity), custom_call_target="tpu_custom_call" | custom-call | tf_op jit(solution)/shard_map/pallas_call | solution.py:445

commit v4 on v3

--- a/solution.py
+++ b/solution.py
@@ -54,7 +54,7 @@
 def step_kernel(
     subdomains, groups,
     vel, prs, fld, brn, advanced, out_vel,
-    cur, noise, now32, next32, vbuf, pbuf, grads, tx, rx,
+    cur, noise, now32, next32, vbuf, pbuf, grads, stress, terms, tx, rx,
     load_sem, flow_sem, vel_send, vel_mates, vel_cross, con_send, con_recv, ready,
 ):
     rows = vel.shape[1]
@@ -181,20 +181,19 @@
     @pl.when(sends_prev)
     def _():
         pl.semaphore_wait(barrier, groups)
-        for f in reversed(range(groups)):
+        for f in sorted(range(groups), key=lambda f: (f % 2, -f)):
             flow_copy((sub - 1, f), groups + 1, vel_cross.at[1]).start()
 
     @pl.when(sends_next)
     def _():
         pl.semaphore_wait(barrier, groups)
-        for f in range(groups):
+        for f in sorted(range(groups), key=lambda f: (f % 2, f)):
             flow_copy((sub + 1, f), 0, vel_cross.at[0]).start()
 
     for number in range(EARLY_CHUNKS, CHUNKS):
         base_chunk(number)
 
     factor = polymer_viscosity / weissenberg
-    stress = {}
 
     scale = 0.5 * time_step
 
@@ -229,6 +228,95 @@
             value = acc[k] * (factor * max_stretch / (count * groups))
             stress[q, k] = value - factor / groups if k in diagonal_pairs else value
 
+    across = (
+        lax.broadcasted_iota(jnp.int32, (rows, LANES), 0) * (LANES // NZ)
+        + lax.broadcasted_iota(jnp.int32, (rows, LANES), 1) // NZ
+    )
+    solid = jnp.where((across < NY // 4) | (across >= NY - NY // 4), 1.0, 0.0)
+    first, last = -reach * groups, groups - 1 + reach * groups
+    mine = [jnp.where(own == q, 1.0, 0.0) for q in range(groups)]
+    y_plus, y_minus, z_plus, z_minus = plane_shifts(pbuf[...])
+    pressure_slopes = (None, y_plus - y_minus, z_plus - z_minus)
+    for a in range(3):
+        mid = vbuf[own + 1, a]
+        y_plus, y_minus, z_plus, z_minus = plane_shifts(mid)
+        terms[a] = transverse_weight * ((y_plus + y_minus) + (z_plus + z_minus))
+        value = mid * (1.0 / time_step)
+        terms[3 + a] = value if a == 0 else value - 0.5 * pressure_slopes[a]
+
+    def fluid(d):
+        plane = sub * groups + d
+        exists = jnp.where((plane >= 0) & (plane < total), 1.0 / diagonal_weight, 0.0)
+        narrow = jnp.where(plane >= total // 2, 1.0, 0.0)
+        return exists * (1.0 - narrow * solid)
+
+    def momentum(outputs):
+        needs = {SWEEPS: sorted(outputs)}
+        for sweep in range(SWEEPS, 1, -1):
+            around = {d + e for d in needs[sweep] for e in (-1, 0, 1)}
+            needs[sweep - 1] = sorted(
+                d for d in around if -sweep < d < groups + sweep - 1
+            )
+        scale_of = {}
+        source = {}
+        start = {}
+        for d in sorted({d for ds in needs.values() for d in ds}):
+            scale_of[d] = fluid(d)
+            if not -1 <= d <= groups:
+                continue
+            along_y = {}
+            along_z = {}
+            if 0 <= d < groups:
+                for k in range(1, 6):
+                    y_plus, y_minus, z_plus, z_minus = plane_shifts(stress[d, k])
+                    along_y[k] = y_plus - y_minus
+                    along_z[k] = z_plus - z_minus
+            for a in range(3):
+                slope = None
+                beside = 0.0
+                for e, sign in ((1, 1.0), (-1, -1.0)):
+                    if 0 <= d + e < groups:
+                        other = stress[d + e, a]
+                        if a == 0:
+                            other = other - mine[d + e] * pbuf[...]
+                        slope = add(slope, sign * other)
+                        beside = beside + mine[d + e]
+                if 0 <= d < groups:
+                    slope = add(slope, along_y[index_table[a][1]] + along_z[index_table[a][2]])
+                value = 0.5 * slope
+                begin = (axial_weight * beside) * vbuf[own + 1, a]
+                if 0 <= d < groups:
+                    value = value + mine[d] * terms[3 + a]
+                    begin = begin + mine[d] * terms[a]
+                source[d, a] = scale_of[d] * value
+                start[d, a] = source[d, a] + scale_of[d] * begin
+        pull = {d: value * transverse_weight for d, value in scale_of.items()}
+        ratio = axial_weight / transverse_weight
+        v = {(d, a): start[d, a] for d in needs[1] for a in range(3)}
+        for sweep in range(2, SWEEPS + 1):
+            fresh = {}
+            for d in needs[sweep]:
+                for a in range(3):
+                    value = add(v.get((d + 1, a)), v.get((d - 1, a)))
+                    if value is not None:
+                        value = value * ratio
+                    if (d, a) in v:
+                        y_plus, y_minus, z_plus, z_minus = plane_shifts(v[d, a])
+                        value = add(value, (y_plus + y_minus) + (z_plus + z_minus))
+                    fresh[d, a] = add(source.get((d, a)), pull[d] * value)
+            v = fresh
+        for d in outputs:
+            for a in range(3):
+                tx[d - first, a] = v[d, a]
+
+    def share(shift, f):
+        return pltpu.make_async_remote_copy(
+            src_ref=tx.at[(reach + shift) * groups + f],
+            dst_ref=rx.at[(reach - shift) * groups + own],
+            send_sem=con_send.at[0], recv_sem=con_recv.at[0],
+            device_id=(sub + shift, f), device_id_type=pl.DeviceIdType.MESH,
+        )
+
     pltpu.make_async_copy(
         vbuf.at[pl.ds(0, groups - 1)], vbuf.at[pl.ds(0, groups - 1)], vel_mates.at[0]
     ).wait()
@@ -246,101 +334,39 @@
 
     plane_fields(0)
 
-    @pl.when(has_next)
-    def _():
-        pltpu.make_async_copy(vbuf.at[0], vbuf.at[0], vel_cross.at[1]).wait()
-
-    plane_fields(groups - 1)
-
-    across = (
-        lax.broadcasted_iota(jnp.int32, (rows, LANES), 0) * (LANES // NZ)
-        + lax.broadcasted_iota(jnp.int32, (rows, LANES), 1) // NZ
-    )
-    solid = jnp.where((across < NY // 4) | (across >= NY - NY // 4), 1.0, 0.0)
-    first, last = -reach * groups, groups - 1 + reach * groups
-    fluid = {}
-    for d in range(first, last + 1):
-        plane = sub * groups + d
-        exists = jnp.where((plane >= 0) & (plane < total), 1.0 / diagonal_weight, 0.0)
-        narrow = jnp.where(plane >= total // 2, 1.0, 0.0)
-        fluid[d] = exists * (1.0 - narrow * solid)
-    pull = {d: value * transverse_weight for d, value in fluid.items()}
-
-    mine = [jnp.where(own == q, 1.0, 0.0) for q in range(groups)]
-    own_vel = [vbuf[own + 1, a] for a in range(3)]
-    own_prs = pbuf[...]
-    y_plus, y_minus, z_plus, z_minus = plane_shifts(own_prs)
-    own_source = [
-        own_vel[0] * (1.0 / time_step),
-        own_vel[1] * (1.0 / time_step) - 0.5 * (y_plus - y_minus),
-        own_vel[2] * (1.0 / time_step) - 0.5 * (z_plus - z_minus),
-    ]
-    sources = {}
-    for d in range(-1, groups + 1):
-        along_y = {}
-        along_z = {}
-        if 0 <= d < groups:
-            for k in range(1, 6):
-                y_plus, y_minus, z_plus, z_minus = plane_shifts(stress[d, k])
-                along_y[k] = y_plus - y_minus
-                along_z[k] = z_plus - z_minus
-        for a in range(3):
-            slope = None
-            if 0 <= d + 1 < groups:
-                above = stress[d + 1, a]
-                if a == 0:
-                    above = above - mine[d + 1] * own_prs
-                slope = above
-            if 0 <= d - 1 < groups:
-                below = stress[d - 1, a]
-                if a == 0:
-                    below = below - mine[d - 1] * own_prs
-                slope = -below if slope is None else slope - below
-            if 0 <= d < groups:
-                slope = slope + along_y[index_table[a][1]] + along_z[index_table[a][2]]
-            value = 0.5 * slope
-            if 0 <= d < groups:
-                value = value + mine[d] * own_source[a]
-            sources[d, a] = value
-
-    v = {(q, a): mine[q] * own_vel[a] for q in range(groups) for a in range(3)}
-    scaled = {(d, a): fluid[d] * value for (d, a), value in sources.items()}
-    ratio = axial_weight / transverse_weight
-    for sweep in range(1, SWEEPS + 1):
-        fresh = {}
-        for d in range(-sweep, groups + sweep):
-            for a in range(3):
-                value = add(v.get((d + 1, a)), v.get((d - 1, a)))
-                if value is not None:
-                    value = value * ratio
-                if (d, a) in v:
-                    y_plus, y_minus, z_plus, z_minus = plane_shifts(v[d, a])
-                    value = add(value, (y_plus + y_minus) + (z_plus + z_minus))
-                fresh[d, a] = add(scaled.get((d, a)), pull[d] * value)
-        v = fresh
-    for d in range(first, last + 1):
-        for a in range(3):
-            tx[d - first, a] = v[d, a] if (d, a) in v else jnp.zeros((rows, LANES), jnp.float32)
-
-    def share(shift, f):
-        return pltpu.make_async_remote_copy(
-            src_ref=tx.at[(reach + shift) * groups + f],
-            dst_ref=rx.at[(reach - shift) * groups + own],
-            send_sem=con_send.at[0], recv_sem=con_recv.at[0],
-            device_id=(sub + shift, f), device_id_type=pl.DeviceIdType.MESH,
-        )
-
     half = max(1, groups // 2)
     across_first = (own // half + 1) * half
-    for shift in range(-reach, reach + 1):
-        if shift != 0:
-            @pl.when(inside(shift))
-            def _(shift=shift):
-                for r in range(groups):
-                    share(shift, (across_first + r) % groups).start()
-        else:
-            for r in range(1, groups):
-                share(0, (own + r) % groups).start()
+    early = groups - 1 - SWEEPS - first
+
+    @pl.when(has_prev)
+    def _():
+        momentum(range(first, first + early))
+        for r in range(groups):
+            f = (across_first + r) % groups
+
+            @pl.when(f < early)
+            def _(f=f):
+                share(-reach, f).start()
+
+    @pl.when(has_next)
+    def _():
+        pltpu.make_async_copy(vbuf.at[0], vbuf.at[0], vel_cross.at[1]).wait()
+
+    plane_fields(groups - 1)
+    momentum(range(first + early, last + 1))
+
+    @pl.when(has_prev)
+    def _():
+        for f in range(early, groups):
+            share(-reach, f).start()
+
+    @pl.when(has_next)
+    def _():
+        for r in range(groups):
+            share(reach, (across_first + r) % groups).start()
+
+    for r in range(1, groups):
+        share(0, (own + r) % groups).start()
 
     here = reach * groups + own
     rx[here] = tx[here]
@@ -417,6 +443,8 @@
             pltpu.VMEM((groups + 2, 3, rows, LANES), jnp.float32),
             pltpu.VMEM((rows, LANES), jnp.float32),
             pltpu.VMEM((groups, 6, rows, LANES), jnp.float32),
+            pltpu.VMEM((groups, 6, rows, LANES), jnp.float32),
+            pltpu.VMEM((6, rows, LANES), jnp.float32),
             pltpu.VMEM((slots, 3, rows, LANES), jnp.float32),
             pltpu.VMEM((slots, 3, rows, LANES), jnp.float32),
             dma((CHUNKS,)),

time: 14.3 us -> 13 us (0.909)
  Pallas kernels: 13.4 us -> 12.1 us
    pallas_call x1, Pallas kernels: 12.3 us -> 11 us  [body(): pl.pallas_call(functools.partial(step_kernel, subdomains, groups), out_sh...]
where the time goes in v4:
time: 13 us; the launch traced here: 12.8 us
  Pallas kernels  12.1 us (93%)
  between operations  0.64 us (5%)
    pallas_call x1, Pallas kernels, body(): pl.pallas_call(functools.partial(step_kernel, subdomains, groups), out_sh...  11 us
    pallas_call x1, Pallas kernels, body(): pl.pallas_call(write_kernel, out_shape=(jax.ShapeDtypeStruct((3, count, p...  1.17 us

profile of v4, /device:TPU:0, one launch (start us, length us, event | category | flops | bytes accessed | tf_op | source)
XLA Modules:
  0.0 12.8 jit_solution(12861573548717105068)
XLA Ops:
  0.6 11.0 %shard_map.59 = (bf16[3,64,32,128]{3,2,1,0:T(8,128)(2,1)S(1)}, f32[3,8,128]{2,1,0:T(8,128)S(1)}) custom-call(f32[3,8,128]{2,1,0:T(8,128)} %bitcast.20, f32[8,128]{1,0:T(8,128)} %bitcast.21, bf16[3,64,32,128]{3,2,1,0:T(8,128)(2,1)} %bitcast.18, bf16[3,64,32,128]{3,2,1,0:T(8,128)(2,1)} %bitcast.19), custom_call_target="tpu_custom_call" | custom-call | tf_op jit(solution)/shard_map/pallas_call | solution.py:430
  11.6 1.2 %shard_map.60 = (bf16[3,64,32,128]{3,2,1,0:T(8,128)(2,1)}, f32[3,8,128]{2,1,0:T(8,128)}) custom-call(bf16[3,64,32,128]{3,2,1,0:T(8,128)(2,1)S(1)} %get-tuple-element.6.advanced, f32[3,8,128]{2,1,0:T(8,128)S(1)} %get-tuple-element.7.velocity), custom_call_target="tpu_custom_call" | custom-call | tf_op jit(solution)/shard_map/pallas_call | solution.py:473

commit v5 on v4

--- a/solution.py
+++ b/solution.py
@@ -95,10 +95,16 @@
     def _():
         greet((sub - 1, groups - 1))
 
-    for helper in range(1, groups - 1):
-        @pl.when(own != helper)
-        def _(helper=helper):
-            greet((sub, helper))
+    for f in range(groups):
+        gathers = own != f
+        if f == 0:
+            gathers = gathers & jnp.logical_not(has_prev)
+        if f == groups - 1:
+            gathers = gathers & jnp.logical_not(has_next)
+
+        @pl.when(gathers)
+        def _(f=f):
+            greet((sub, f))
 
     for number in range(CHUNKS):
         part = pl.ds(number * chunk, chunk)
@@ -144,27 +150,28 @@
     for number in range(EARLY_CHUNKS):
         base_chunk(number)
 
-    for copy in flow_loads:
-        copy.wait()
     sends_prev = (own == 0) & has_prev
     sends_next = (own == groups - 1) & has_next
-    edge = (own == 0) | (own == groups - 1)
-
-    @pl.when(jnp.logical_not(edge))
+    guided = sends_prev | sends_next
+
+    @pl.when(jnp.logical_not(guided))
     def _():
         pl.semaphore_wait(barrier, groups - 1)
 
-    def admit(helper, device):
-        @pl.when(own == helper)
+    def admit(helper, device, needed):
+        @pl.when((own == helper) & needed)
         def _():
             pl.semaphore_signal(
                 ready, inc=1, device_id=(sub, device), device_id_type=pl.DeviceIdType.MESH
             )
 
-    admit(1, 0)
-    admit(groups - 2, groups - 1)
-
-    @pl.when(edge)
+    admit(1, 0, has_prev)
+    admit(groups - 2, groups - 1, has_next)
+
+    for copy in flow_loads:
+        copy.wait()
+
+    @pl.when(guided)
     def _():
         pl.semaphore_wait(ready, 1)
 
@@ -175,8 +182,18 @@
             device_id=device, device_id_type=pl.DeviceIdType.MESH,
         )
 
-    for r in range(1, groups):
-        flow_copy((sub, (own + r) % groups), own + 1, vel_mates.at[0]).start()
+    half = max(1, groups // 2)
+    across_first = (own // half + 1) * half
+
+    def to_mates(send):
+        for r in range(groups):
+            f = (across_first + r) % groups
+
+            @pl.when(f != own)
+            def _(f=f):
+                send(f).start()
+
+    to_mates(lambda f: flow_copy((sub, f), own + 1, vel_mates.at[0]))
 
     @pl.when(sends_prev)
     def _():
@@ -334,17 +351,17 @@
 
     plane_fields(0)
 
-    half = max(1, groups // 2)
-    across_first = (own // half + 1) * half
     early = groups - 1 - SWEEPS - first
 
     @pl.when(has_prev)
     def _():
-        momentum(range(first, first + early))
+        momentum([first])
+        share(-reach, 0).start()
+        momentum(range(first + 1, first + early))
         for r in range(groups):
             f = (across_first + r) % groups
 
-            @pl.when(f < early)
+            @pl.when((f > 0) & (f < early))
             def _(f=f):
                 share(-reach, f).start()
 
@@ -353,20 +370,27 @@
         pltpu.make_async_copy(vbuf.at[0], vbuf.at[0], vel_cross.at[1]).wait()
 
     plane_fields(groups - 1)
-    momentum(range(first + early, last + 1))
+    def share_next():
+        for r in range(groups):
+            share(reach, (across_first + r) % groups).start()
 
     @pl.when(has_prev)
     def _():
+        @pl.when(has_next)
+        def _():
+            momentum(range(groups, last + 1))
+            share_next()
+
+        momentum(range(first + early, groups))
         for f in range(early, groups):
             share(-reach, f).start()
-
-    @pl.when(has_next)
-    def _():
-        for r in range(groups):
-            share(reach, (across_first + r) % groups).start()
-
-    for r in range(1, groups):
-        share(0, (own + r) % groups).start()
+        to_mates(lambda f: share(0, f))
+
+    @pl.when(jnp.logical_not(has_prev))
+    def _():
+        momentum(range(0, last + 1))
+        to_mates(lambda f: share(0, f))
+        pl.when(has_next)(share_next)
 
     here = reach * groups + own
     rx[here] = tx[here]

time: 13 us -> 12.8 us (0.985)
    pallas_call x1, Pallas kernels: 11 us -> 10.8 us  [body(): pl.pallas_call(functools.partial(step_kernel, subdomains, groups), out_sh...]
where the time goes in v5:
time: 12.8 us; the launch traced here: 12.6 us
  Pallas kernels  12 us (94%)
  between operations  0.64 us (5%)
    pallas_call x1, Pallas kernels, body(): pl.pallas_call(functools.partial(step_kernel, subdomains, groups), out_sh...  10.8 us
    pallas_call x1, Pallas kernels, body(): pl.pallas_call(write_kernel, out_shape=(jax.ShapeDtypeStruct((3, count, p...  1.17 us

profile of v5, /device:TPU:0, one launch (start us, length us, event | category | flops | bytes accessed | tf_op | source)
XLA Modules:
  0.0 12.6 jit_solution(15918147157094750309)
XLA Ops:
  0.6 10.8 %shard_map.59 = (bf16[3,64,32,128]{3,2,1,0:T(8,128)(2,1)S(1)}, f32[3,8,128]{2,1,0:T(8,128)S(1)}) custom-call(f32[3,8,128]{2,1,0:T(8,128)} %bitcast.20, f32[8,128]{1,0:T(8,128)} %bitcast.21, bf16[3,64,32,128]{3,2,1,0:T(8,128)(2,1)} %bitcast.18, bf16[3,64,32,128]{3,2,1,0:T(8,128)(2,1)} %bitcast.19), custom_call_target="tpu_custom_call" | custom-call | tf_op jit(solution)/shard_map/pallas_call | solution.py:454
  11.4 1.2 %shard_map.60 = (bf16[3,64,32,128]{3,2,1,0:T(8,128)(2,1)}, f32[3,8,128]{2,1,0:T(8,128)}) custom-call(bf16[3,64,32,128]{3,2,1,0:T(8,128)(2,1)S(1)} %get-tuple-element.6.advanced, f32[3,8,128]{2,1,0:T(8,128)S(1)} %get-tuple-element.7.velocity), custom_call_target="tpu_custom_call" | custom-call | tf_op jit(solution)/shard_map/pallas_call | solution.py:497

commit v6 on v5

--- a/solution.py
+++ b/solution.py
@@ -11,7 +11,7 @@
 NZ = 32
 SWEEPS = 4
 LANES = 128
-CHUNKS = 4
+CHUNKS = 2
 EARLY_CHUNKS = 0
 UNROLL = 32
 VMEM_LIMIT = 24 * 1024 * 1024
@@ -55,7 +55,7 @@
     subdomains, groups,
     vel, prs, fld, brn, advanced, out_vel,
     cur, noise, now32, next32, vbuf, pbuf, grads, stress, terms, tx, rx,
-    load_sem, flow_sem, vel_send, vel_mates, vel_cross, con_send, con_recv, ready,
+    load_sem, flow_sem, send_sem, vel_mates, vel_cross, con_recv, ready,
 ):
     rows = vel.shape[1]
     count = fld.shape[1]
@@ -75,7 +75,7 @@
 
     flow_loads = [
         pltpu.make_async_copy(vel, vbuf.at[own + 1], flow_sem.at[0]),
-        pltpu.make_async_copy(prs, pbuf, flow_sem.at[1]),
+        pltpu.make_async_copy(prs, pbuf, flow_sem.at[0]),
     ]
     for copy in flow_loads:
         copy.start()
@@ -133,8 +133,8 @@
     relax = time_step * max_stretch / (2.0 * weissenberg)
 
     def base_chunk(number):
-        both = pl.ds(0, 2 * chunk)
-        pltpu.make_async_copy(fld.at[:, both], cur.at[:, both], load_sem.at[number]).wait()
+        both = now32.at[:, pl.ds(0, chunk)]
+        pltpu.make_async_copy(both, both, load_sem.at[number]).wait()
 
         @pl.loop(number * chunk, (number + 1) * chunk, unroll=2)
         def _(n):
@@ -168,8 +168,8 @@
     admit(1, 0, has_prev)
     admit(groups - 2, groups - 1, has_next)
 
-    for copy in flow_loads:
-        copy.wait()
+    loaded = stress.at[0, pl.ds(0, 4)]
+    pltpu.make_async_copy(loaded, loaded, flow_sem.at[0]).wait()
 
     @pl.when(guided)
     def _():
@@ -178,7 +178,7 @@
     def flow_copy(device, slot, recv):
         return pltpu.make_async_remote_copy(
             src_ref=vbuf.at[own + 1], dst_ref=vbuf.at[slot],
-            send_sem=vel_send.at[0], recv_sem=recv,
+            send_sem=send_sem.at[0], recv_sem=recv,
             device_id=device, device_id_type=pl.DeviceIdType.MESH,
         )
 
@@ -193,7 +193,8 @@
             def _(f=f):
                 send(f).start()
 
-    to_mates(lambda f: flow_copy((sub, f), own + 1, vel_mates.at[0]))
+    arrives = vel_mates.at[jnp.where(own == 0, 1, 0)]
+    to_mates(lambda f: flow_copy((sub, f), own + 1, arrives))
 
     @pl.when(sends_prev)
     def _():
@@ -330,20 +331,50 @@
         return pltpu.make_async_remote_copy(
             src_ref=tx.at[(reach + shift) * groups + f],
             dst_ref=rx.at[(reach - shift) * groups + own],
-            send_sem=con_send.at[0], recv_sem=con_recv.at[0],
+            send_sem=send_sem.at[0], recv_sem=con_recv.at[0],
             device_id=(sub + shift, f), device_id_type=pl.DeviceIdType.MESH,
         )
 
-    pltpu.make_async_copy(
-        vbuf.at[pl.ds(0, groups - 1)], vbuf.at[pl.ds(0, groups - 1)], vel_mates.at[0]
-    ).wait()
-    for q in range(groups):
-        for a in range(3):
-            y_plus, y_minus, z_plus, z_minus = plane_shifts(vbuf[q + 1, a])
-            grads[q, a] = (y_plus - y_minus) * scale
-            grads[q, 3 + a] = (z_plus - z_minus) * scale
-    for q in range(1, groups - 1):
+    def wait_velocity(number, sem):
+        planes = vbuf.at[pl.ds(0, number)]
+        pltpu.make_async_copy(planes, planes, sem).wait()
+
+    def cross_slopes(planes):
+        for q in planes:
+            for a in range(3):
+                y_plus, y_minus, z_plus, z_minus = plane_shifts(vbuf[q + 1, a])
+                grads[q, a] = (y_plus - y_minus) * scale
+                grads[q, 3 + a] = (z_plus - z_minus) * scale
+
+    @pl.when(own == 0)
+    def _():
+        wait_velocity(groups - 1, vel_mates.at[0])
+
+    @pl.when(own != 0)
+    def _():
+        wait_velocity(groups - 2, vel_mates.at[0])
+
+    @pl.when((own != 0) & (own < half))
+    def _():
+        wait_velocity(1, vel_mates.at[1])
+
+    @pl.when(own < half)
+    def _():
+        cross_slopes(range(groups))
+
+    @pl.when(own >= half)
+    def _():
+        cross_slopes(range(1, groups))
+
+    for q in reversed(range(2, groups - 1)):
         plane_fields(q)
+
+    @pl.when(own >= half)
+    def _():
+        wait_velocity(1, vel_mates.at[1])
+        cross_slopes(range(1))
+
+    plane_fields(1)
 
     @pl.when(has_prev)
     def _():
@@ -388,9 +419,13 @@
 
     @pl.when(jnp.logical_not(has_prev))
     def _():
-        momentum(range(0, last + 1))
+        momentum(range(0, groups))
         to_mates(lambda f: share(0, f))
-        pl.when(has_next)(share_next)
+
+        @pl.when(has_next)
+        def _():
+            momentum(range(groups, last + 1))
+            share_next()
 
     here = reach * groups + own
     rx[here] = tx[here]
@@ -412,19 +447,20 @@
         for option in options:
             @pl.when(number == option)
             def _(option=option):
-                planes = rx.at[pl.ds(0, option)]
+                planes = now32.at[:, pl.ds(0, option), pl.ds(0, rows)]
                 pltpu.make_async_copy(planes, planes, sem).wait()
 
-    flow_options = [groups - 1 + k * groups for k in range(3)]
-    share_options = [groups - 1 + k * groups for k in range(spread)]
-    wait_planes(sent_flow, flow_options, vel_send.at[0])
-    wait_planes(partners, share_options, con_recv.at[0])
+    wait_planes(partners, [groups - 1 + k * groups for k in range(spread)], con_recv.at[0])
     for a in range(3):
         value = rx[0, a]
         for k in range(1, spread * groups):
             value = value + rx[k, a]
         out_vel[a] = value
-    wait_planes(partners, share_options, con_send.at[0])
+    wait_planes(
+        partners + sent_flow,
+        [2 * (groups - 1) + k * groups for k in range(spread + 1)],
+        send_sem.at[0],
+    )
 
 
 def write_kernel(advanced, velocity, out_fields, out_vel, out_sem):
@@ -472,11 +508,10 @@
             pltpu.VMEM((slots, 3, rows, LANES), jnp.float32),
             pltpu.VMEM((slots, 3, rows, LANES), jnp.float32),
             dma((CHUNKS,)),
-            dma((2,)),
             dma((1,)),
             dma((1,)),
             dma((2,)),
-            dma((1,)),
+            dma((2,)),
             dma((1,)),
             pltpu.SemaphoreType.REGULAR,
         ],

time: 12.8 us -> 12.5 us (0.977)
  Pallas kernels: 12 us -> 11.8 us
    pallas_call x1, Pallas kernels: 10.8 us -> 10.6 us  [body(): pl.pallas_call(functools.partial(step_kernel, subdomains, groups), out_sh...]
where the time goes in v6:
time: 12.5 us; the launch traced here: 12.4 us
  Pallas kernels  11.8 us (94%)
  between operations  0.64 us (5%)
    pallas_call x1, Pallas kernels, body(): pl.pallas_call(functools.partial(step_kernel, subdomains, groups), out_sh...  10.6 us
    pallas_call x1, Pallas kernels, body(): pl.pallas_call(write_kernel, out_shape=(jax.ShapeDtypeStruct((3, count, p...  1.17 us

profile of v6, /device:TPU:0, one launch (start us, length us, event | category | flops | bytes accessed | tf_op | source)
XLA Modules:
  0.0 12.4 jit_solution(3644415902661467267)
XLA Ops:
  0.6 10.6 %shard_map.59 = (bf16[3,64,32,128]{3,2,1,0:T(8,128)(2,1)S(1)}, f32[3,8,128]{2,1,0:T(8,128)S(1)}) custom-call(f32[3,8,128]{2,1,0:T(8,128)} %bitcast.20, f32[8,128]{1,0:T(8,128)} %bitcast.21, bf16[3,64,32,128]{3,2,1,0:T(8,128)(2,1)} %bitcast.18, bf16[3,64,32,128]{3,2,1,0:T(8,128)(2,1)} %bitcast.19), custom_call_target="tpu_custom_call" | custom-call | tf_op jit(solution)/shard_map/pallas_call | solution.py:490
  11.2 1.2 %shard_map.60 = (bf16[3,64,32,128]{3,2,1,0:T(8,128)(2,1)}, f32[3,8,128]{2,1,0:T(8,128)}) custom-call(bf16[3,64,32,128]{3,2,1,0:T(8,128)(2,1)S(1)} %get-tuple-element.6.advanced, f32[3,8,128]{2,1,0:T(8,128)S(1)} %get-tuple-element.7.velocity), custom_call_target="tpu_custom_call" | custom-call | tf_op jit(solution)/shard_map/pallas_call | solution.py:532

commit v7 on v6

--- a/solution.py
+++ b/solution.py
@@ -215,21 +215,41 @@
 
     scale = 0.5 * time_step
 
-    def plane_fields(q):
+    def prepare_fields(q):
         g = [None] * 9
         for a in range(3):
+            g[3 * a] = vbuf[q, a] * -scale
+            g[3 * a + 1] = grads[q, a]
+            g[3 * a + 2] = grads[q, 3 + a]
+        at = pl.ds(q, rows, stride=groups)
+
+        @pl.loop(0, count, unroll=UNROLL // 2)
+        def _(n):
+            now = [now32[c, n, at] for c in range(3)]
+            for a in range(3):
+                next32[a, n, at] = next32[a, n, at] + (
+                    g[3 * a] * now[0] + g[3 * a + 1] * now[1] + g[3 * a + 2] * now[2]
+                )
+
+    def plane_fields(q, prepared=False):
+        g = [None] * 9
+        for a in range(3):
+            if prepared:
+                g[3 * a] = vbuf[q + 2, a] * scale
+                continue
             g[3 * a] = (vbuf[q + 2, a] - vbuf[q, a]) * scale
             g[3 * a + 1] = grads[q, a]
             g[3 * a + 2] = grads[q, 3 + a]
         at = pl.ds(q, rows, stride=groups)
 
         def one_field(n, acc):
-            now = [now32[c, n, at] for c in range(3)]
+            now = [now32[c, n, at] for c in range(1 if prepared else 3)]
             new = []
             for a in range(3):
-                value = next32[a, n, at] + (
-                    g[3 * a] * now[0] + g[3 * a + 1] * now[1] + g[3 * a + 2] * now[2]
-                )
+                stretch = g[3 * a] * now[0]
+                if not prepared:
+                    stretch = stretch + g[3 * a + 1] * now[1] + g[3 * a + 2] * now[2]
+                value = next32[a, n, at] + stretch
                 next32[a, n, at] = value
                 new.append(value)
             square = new[0] * new[0] + new[1] * new[1] + new[2] * new[2]
@@ -396,11 +416,13 @@
             def _(f=f):
                 share(-reach, f).start()
 
+    prepare_fields(groups - 1)
+
     @pl.when(has_next)
     def _():
         pltpu.make_async_copy(vbuf.at[0], vbuf.at[0], vel_cross.at[1]).wait()
 
-    plane_fields(groups - 1)
+    plane_fields(groups - 1, True)
     def share_next():
         for r in range(groups):
             share(reach, (across_first + r) % groups).start()

time: 12.5 us -> 12.4 us (level)
  Pallas kernels: 11.8 us -> 11.6 us
    pallas_call x1, Pallas kernels: 10.6 us -> 10.4 us  [body(): pl.pallas_call(functools.partial(step_kernel, subdomains, groups), out_sh...]
where the time goes in v7:
time: 12.4 us; the launch traced here: 12.2 us
  Pallas kernels  11.6 us (94%)
  between operations  0.64 us (5%)
    pallas_call x1, Pallas kernels, body(): pl.pallas_call(functools.partial(step_kernel, subdomains, groups), out_sh...  10.4 us
    pallas_call x1, Pallas kernels, body(): pl.pallas_call(write_kernel, out_shape=(jax.ShapeDtypeStruct((3, count, p...  1.17 us

profile of v7, /device:TPU:0, one launch (start us, length us, event | category | flops | bytes accessed | tf_op | source)
XLA Modules:
  0.0 12.2 jit_solution(17555144721002462453)
XLA Ops:
  0.6 10.4 %shard_map.59 = (bf16[3,64,32,128]{3,2,1,0:T(8,128)(2,1)S(1)}, f32[3,8,128]{2,1,0:T(8,128)S(1)}) custom-call(f32[3,8,128]{2,1,0:T(8,128)} %bitcast.20, f32[8,128]{1,0:T(8,128)} %bitcast.21, bf16[3,64,32,128]{3,2,1,0:T(8,128)(2,1)} %bitcast.18, bf16[3,64,32,128]{3,2,1,0:T(8,128)(2,1)} %bitcast.19), custom_call_target="tpu_custom_call" | custom-call | tf_op jit(solution)/shard_map/pallas_call | solution.py:512
  11.0 1.2 %shard_map.60 = (bf16[3,64,32,128]{3,2,1,0:T(8,128)(2,1)}, f32[3,8,128]{2,1,0:T(8,128)}) custom-call(bf16[3,64,32,128]{3,2,1,0:T(8,128)(2,1)S(1)} %get-tuple-element.6.advanced, f32[3,8,128]{2,1,0:T(8,128)S(1)} %get-tuple-element.7.velocity), custom_call_target="tpu_custom_call" | custom-call | tf_op jit(solution)/shard_map/pallas_call | solution.py:554

commit v8 on v7

--- a/solution.py
+++ b/solution.py
@@ -288,12 +288,12 @@
         narrow = jnp.where(plane >= total // 2, 1.0, 0.0)
         return exists * (1.0 - narrow * solid)
 
-    def momentum(outputs):
+    def momentum(outputs, lowest=first):
         needs = {SWEEPS: sorted(outputs)}
         for sweep in range(SWEEPS, 1, -1):
             around = {d + e for d in needs[sweep] for e in (-1, 0, 1)}
             needs[sweep - 1] = sorted(
-                d for d in around if -sweep < d < groups + sweep - 1
+                d for d in around if max(-sweep, lowest - 1) < d < groups + sweep - 1
             )
         scale_of = {}
         source = {}
@@ -424,7 +424,7 @@
 
     plane_fields(groups - 1, True)
     def share_next():
-        for r in range(groups):
+        for r in sorted(range(groups), key=lambda r: (r // half, -r)):
             share(reach, (across_first + r) % groups).start()
 
     @pl.when(has_prev)
@@ -441,12 +441,12 @@
 
     @pl.when(jnp.logical_not(has_prev))
     def _():
-        momentum(range(0, groups))
+        momentum(range(0, groups), 0)
         to_mates(lambda f: share(0, f))
 
         @pl.when(has_next)
         def _():
-            momentum(range(groups, last + 1))
+            momentum(range(groups, last + 1), 0)
             share_next()
 
     here = reach * groups + own
@@ -487,8 +487,8 @@
 
 def write_kernel(advanced, velocity, out_fields, out_vel, out_sem):
     copies = [
+        pltpu.make_async_copy(advanced, out_fields, out_sem.at[0]),
         pltpu.make_async_copy(velocity, out_vel, out_sem.at[1]),
-        pltpu.make_async_copy(advanced, out_fields, out_sem.at[0]),
     ]
     for copy in copies:
         copy.start()

time: 12.4 us -> 12.4 us (level)
  no operation moved by 1% of the time
where the time goes in v8:
time: 12.4 us; the launch traced here: 12.2 us
  Pallas kernels  11.6 us (94%)
  between operations  0.64 us (5%)
    pallas_call x1, Pallas kernels, body(): pl.pallas_call(functools.partial(step_kernel, subdomains, groups), out_sh...  10.4 us
    pallas_call x1, Pallas kernels, body(): pl.pallas_call(write_kernel, out_shape=(jax.ShapeDtypeStruct((3, count, p...  1.16 us

profile of v8, /device:TPU:0, one launch (start us, length us, event | category | flops | bytes accessed | tf_op | source)
XLA Modules:
  0.0 12.2 jit_solution(4305814974319201902)
XLA Ops:
  0.6 10.4 %shard_map.59 = (bf16[3,64,32,128]{3,2,1,0:T(8,128)(2,1)S(1)}, f32[3,8,128]{2,1,0:T(8,128)S(1)}) custom-call(f32[3,8,128]{2,1,0:T(8,128)} %bitcast.20, f32[8,128]{1,0:T(8,128)} %bitcast.21, bf16[3,64,32,128]{3,2,1,0:T(8,128)(2,1)} %bitcast.18, bf16[3,64,32,128]{3,2,1,0:T(8,128)(2,1)} %bitcast.19), custom_call_target="tpu_custom_call" | custom-call | tf_op jit(solution)/shard_map/pallas_call | solution.py:512
  11.0 1.2 %shard_map.60 = (bf16[3,64,32,128]{3,2,1,0:T(8,128)(2,1)}, f32[3,8,128]{2,1,0:T(8,128)}) custom-call(bf16[3,64,32,128]{3,2,1,0:T(8,128)(2,1)S(1)} %get-tuple-element.6.advanced, f32[3,8,128]{2,1,0:T(8,128)S(1)} %get-tuple-element.7.velocity), custom_call_target="tpu_custom_call" | custom-call | tf_op jit(solution)/shard_map/pallas_call | solution.py:554
